TPU v7x, 32 devices: a whole 2x2x4 slice. The times are simulated.
32 devices in a mesh: gy: 16 (over z, y, core), gz: 2 (over x).
Axes of the slice: x: 2, y: 2, z: 4, core: 2. Of those that a mesh axis runs over, the one named last changes fastest.
Arguments:
- omega: float32 [3, 256, 128, 128], P(None, 'gy', 'gz'), may hold values from -6 to 6
- velocity: float32 [3, 256, 128, 128], P(None, 'gy', 'gz'), may hold values from -6 to 6
- point_owner: int32 [1152], replicated, may hold values from 0 to 22, as said below
- point_cells: int32 [3, 1152], replicated, may hold values from 1 to 125, as said below
- point_frac: float32 [3, 1152], replicated, may hold values from 0 to 1
- chord: float32 [1152], replicated, may hold values from 0.2 to 1
- twist: float32 [1152], replicated, may hold values from -0.3 to 0.3
- angle_step: int32 [1], replicated, may hold values from 0 to 719
Outputs:
- omega_out: float32 [3, 256, 128, 128], P(None, 'gy', 'gz')
- blade_sources: float32 [3, 1152], replicated
Inputs may be any that keep to these rules, and one draw needn't show every extreme that they name: `point_owner`: turbine t's points lie in spanwise blocks t * 2 to (t + 1) * 2 - 1 and in the 1 vertical blocks from (1) // 2 on; no block holds more than 192 points, and in every turbine one block holds exactly 192. `point_cells`: streamwise cells lie in 1 to 125, spanwise in 1 to 13, vertical in 1 to 61; all points of a turbine share one streamwise cell.
All inputs are finite; a program needn't handle non-finite values.
Results may differ from a plain program's by a relative error of at most 0.0003.
Values sent between devices are 32-bit elements; how exact they have to be, the bound alone decides.
A program may use at most 128 MiB of HBM per device.

v0:
```python
import jax
import jax.numpy as jnp
from jax import lax
from jax.sharding import PartitionSpec as P

TURBINES = 6
BLADES = 3
BP = 64
section_step = 0.4
viscosity = 0.05
tip_speed = 3.0
turn_step = 2.0 * 3.141592653589793 / 720.0


def with_halo(x, sides, width):
    for axis, dim in sides:
        size, length = (lax.axis_size(axis), x.shape[dim])
        up = [(i, (i + 1) % size) for i in range(size - 1)]
        down = [(j, i) for i, j in up]
        last = lax.slice_in_dim(x, length - width, length, axis=dim)
        initial = lax.slice_in_dim(x, 0, width, axis=dim)
        before = lax.ppermute(last, axis, up)
        after = lax.ppermute(initial, axis, down)
        x = jnp.concatenate([before, x, after], axis=dim)
    return x


def remesh_kernel(shift):
    mag = jnp.abs(shift)
    inner = 1.0 - 2.5 * mag * mag + 1.5 * mag * mag * mag
    outer = 0.5 * (2.0 - mag) * (2.0 - mag) * (1.0 - mag)
    return jnp.where(mag < 1.0, inner, jnp.where(mag < 2.0, outer, 0.0))


def shifted(padded, axis, offset):
    index = []
    for dim in range(4):
        if dim == 0:
            index.append(slice(None))
        elif dim == axis:
            index.append(slice(offset, offset + padded.shape[dim] - 4))
        else:
            index.append(slice(2, padded.shape[dim] - 2))
    return padded[tuple(index)]


def centered_first(padded, axis):
    return (
        shifted(padded, axis, 0)
        - 8.0 * shifted(padded, axis, 1)
        + 8.0 * shifted(padded, axis, 3)
        - shifted(padded, axis, 4)
    ) / 12.0


def centered_second(padded, axis):
    return (
        -shifted(padded, axis, 0)
        + 16.0 * shifted(padded, axis, 1)
        - 30.0 * shifted(padded, axis, 2)
        + 16.0 * shifted(padded, axis, 3)
        - shifted(padded, axis, 4)
    ) / 12.0


def remesh_padded(field, displace, axis):
    length = field.shape[axis] - 4
    total = jnp.zeros(field.shape[:axis] + (length,) + field.shape[axis + 1 :], jnp.float32)
    for offset in range(-2, 3):
        start = 2 - offset
        part = lax.slice_in_dim(field, start, start + length, axis=axis)
        moved = lax.slice_in_dim(displace, start, start + length, axis=axis - 1)
        total = total + remesh_kernel(offset - moved)[None] * part
    return total


def blade_forces(point_velocity, chord, twist, angle_step):
    count = point_velocity.shape[1]
    points = jnp.arange(count, dtype=jnp.int32)
    station = points % BP
    blade = points // BP % BLADES
    theta = angle_step[0].astype(
        jnp.float32
    ) * turn_step + 2.0 * 3.141592653589793 / 3.0 * blade.astype(jnp.float32)
    radius = (station.astype(jnp.float32) + 0.5) / BP
    cos_t = jnp.cos(theta)
    sin_t = jnp.sin(theta)
    rel_x = point_velocity[0]
    rel_y = point_velocity[1] + tip_speed * radius * sin_t
    rel_z = point_velocity[2] - tip_speed * radius * cos_t
    rel_t = -sin_t * rel_y + cos_t * rel_z
    speed = jnp.sqrt(rel_x * rel_x + rel_t * rel_t + 1.0)
    gamma = 3.141592653589793 * chord * (rel_x * jnp.cos(twist) + rel_t * jnp.sin(twist))
    blades = gamma.reshape(-1, BP)
    before = jnp.concatenate([jnp.zeros((blades.shape[0], 1), jnp.float32), blades[:, :-1]], axis=1)
    shed = (blades - before).reshape(-1)
    return jnp.stack(
        [
            shed * rel_x / speed,
            gamma * cos_t + shed * rel_y / speed,
            gamma * sin_t + shed * rel_z / speed,
        ]
    )


def point_tables(
    cells,
    fracs,
    owner_span,
    owner_vert,
    span_index,
    vert_index,
    span_cells,
    vert_cells,
    axial_cells,
):
    rows_x = jnp.arange(axial_cells, dtype=jnp.int32)
    rows_y = jnp.arange(span_cells, dtype=jnp.int32)
    rows_z = jnp.arange(vert_cells, dtype=jnp.int32)
    gap_x = rows_x[:, None] - cells[0][None, :]
    gap_y = (
        span_index * span_cells
        + rows_y[:, None]
        - owner_span[None, :] * span_cells
        - cells[1][None, :]
    )
    gap_z = (
        vert_index * vert_cells
        + rows_z[:, None]
        - owner_vert[None, :] * vert_cells
        - cells[2][None, :]
    )
    table_x = remesh_kernel(gap_x.astype(jnp.float32) - fracs[0][None, :])
    table_y = remesh_kernel(gap_y.astype(jnp.float32) - fracs[1][None, :])
    table_z = remesh_kernel(gap_z.astype(jnp.float32) - fracs[2][None, :])
    return (table_x, table_y, table_z)


def on_device(omega, velocity, point_owner, point_cells, point_frac, chord, twist, angle_step):
    span_cells, vert_cells, axial_cells = (omega.shape[1], omega.shape[2], omega.shape[3])
    span_count = lax.axis_size("gy")
    vert_count = lax.axis_size("gz")
    span_index = lax.axis_index("gy")
    vert_index = lax.axis_index("gz")
    owner_span = point_owner // vert_count
    owner_vert = point_owner % vert_count
    highest = lax.Precision.HIGHEST
    busiest = 2 * (BLADES * BP) // (span_count // TURBINES * max(vert_count // 2, 1))
    my_block = span_index * vert_count + vert_index
    points = jnp.arange(point_owner.shape[0], dtype=jnp.int32)
    ranking = jnp.where(point_owner == my_block, points, points + point_owner.shape[0])
    picked = jnp.argsort(ranking, stable=True)[:busiest]
    selector = (picked[:, None] == points[None, :]).astype(jnp.float32)
    table_x, table_y, table_z = point_tables(
        point_cells[:, picked],
        point_frac[:, picked],
        owner_span[picked],
        owner_vert[picked],
        span_index,
        vert_index,
        span_cells,
        vert_cells,
        axial_cells,
    )
    columns = jnp.dot(
        velocity.reshape(-1, axial_cells),
        table_x,
        precision=highest,
        preferred_element_type=jnp.float32,
    )
    columns = columns.reshape(3, span_cells, vert_cells, -1)
    compact = jnp.einsum("cyzq,yq,zq->cq", columns, table_y, table_z, precision=highest)
    partial_velocity = jnp.dot(
        compact, selector, precision=highest, preferred_element_type=jnp.float32
    )
    point_velocity = lax.psum(partial_velocity, ("gy", "gz"))
    sources = blade_forces(point_velocity, chord, twist, angle_step)
    local_sources = sources[:, picked]
    spread = jnp.einsum("cq,yq,zq->cyzq", local_sources, table_y, table_z, precision=highest)
    smear = jnp.dot(
        spread.reshape(-1, spread.shape[3]),
        table_x.T,
        precision=highest,
        preferred_element_type=jnp.float32,
    )
    smear = smear.reshape(3, span_cells, vert_cells, axial_cells)
    omega_rim, velocity_rim = (
        with_halo(omega, (("gy", 1), ("gz", 2)), 2),
        with_halo(velocity, (("gy", 1), ("gz", 2)), 2),
    )
    axial_pads = ((0, 0), (0, 0), (0, 0), (2, 2))
    omega_pad = jnp.pad(omega_rim, axial_pads)
    velocity_pad = jnp.pad(velocity_rim, axial_pads)
    stretch = jnp.zeros_like(omega)
    laplace = jnp.zeros_like(omega)
    for axis in range(3):
        stretch = stretch + omega[2 - axis][None] * centered_first(velocity_pad, 3 - axis)
        laplace = laplace + centered_second(omega_pad, axis + 1)
    section = omega + section_step * (stretch + viscosity * laplace + smear)
    shift_x = jnp.clip(section_step * velocity[0], -1.0, 1.0)
    moved_x = remesh_padded(
        jnp.pad(section, axial_pads), jnp.pad(shift_x, ((0, 0), (0, 0), (2, 2))), 3
    )
    shift_z = jnp.clip(section_step * velocity_rim[2][2 : span_cells + 2, :, :], -1.0, 1.0)
    span_rim = with_halo(moved_x, (("gy", 1),), 2)
    shift_y = jnp.clip(section_step * velocity_rim[1][:, 2 : vert_cells + 2, :], -1.0, 1.0)
    moved_mid = remesh_padded(span_rim, shift_y, 1)
    moved_y = with_halo(moved_mid, (("gz", 2),), 2)
    omega_out = remesh_padded(moved_y, shift_z, 2)
    return (omega_out, sources)


def solution(mesh):
    in_specs = (P(None, "gy", "gz", None), P(None, "gy", "gz", None), P(), P(), P(), P(), P(), P())
    out_specs = (P(None, "gy", "gz", None), P())
    return jax.shard_map(
        on_device, mesh=mesh, in_specs=in_specs, out_specs=out_specs, check_vma=False
    )
```

profile of v0, /device:TPU:10, one launch (start us, length us, event | category | flops | bytes accessed | tf_op | source)
XLA Modules:
  0.0 163.6 jit_solution(6236119518289551892)
XLA Ops:
  0.6 1.8 %fusion.252 = (f32[3,2,64,128]{3,2,1,0:T(8,128)}, f32[3,2,64,128]{3,2,1,0:T(8,128)}) fusion(f32[3,16,64,128]{3,2,1,0:T(8,128)} %param.9), kind=kLoop, calls=%fused_computation.439 | loop fusion | bytes 786432 | tf_op jit(solution)/shard_map/slice | solution.py:21
  2.5 2.0 %collective-permute-start = (f32[3,2,64,128]{3,2,1,0:T(8,128)}, f32[3,2,64,128]{3,2,1,0:T(8,128)}, u32[]{:S(2)}, u32[]{:S(2)}) collective-permute-start(f32[3,2,64,128]{3,2,1,0:T(8,128)} %get-tuple-element.33), channel_id=1, source_target_pairs={{0,2},{2,4},{4,6},{6,8},{8,10},{10,12},{12,14},{14,16},{16,18},{18... | collective-permute-start | bytes 589832 | tf_op jit(solution)/shard_map/ppermute | solution.py:22
  4.5 4.5 %collective-permute-start.1 = (f32[3,2,64,128]{3,2,1,0:T(8,128)}, f32[3,2,64,128]{3,2,1,0:T(8,128)}, u32[]{:S(2)}, u32[]{:S(2)}) collective-permute-start(f32[3,2,64,128]{3,2,1,0:T(8,128)} %get-tuple-element.32), channel_id=1, source_target_pairs={{2,0},{4,2},{6,4},{8,6},{10,8},{12,10},{14,12},{16,14},{18,16},{20... | collective-permute-start | bytes 589832 | tf_op jit(solution)/shard_map/ppermute | solution.py:23
  9.1 1.7 %fusion.253 = (f32[3,2,64,128]{3,2,1,0:T(8,128)S(1)}, f32[3,2,64,128]{3,2,1,0:T(8,128)}) fusion(f32[3,16,64,128]{3,2,1,0:T(8,128)} %param.8), kind=kLoop, calls=%fused_computation.440 | loop fusion | bytes 786432 | tf_op jit(solution)/shard_map/slice | solution.py:21
  10.8 2.0 %collective-permute-start.4 = (f32[3,2,64,128]{3,2,1,0:T(8,128)}, f32[3,2,64,128]{3,2,1,0:T(8,128)}, u32[]{:S(2)}, u32[]{:S(2)}) collective-permute-start(f32[3,2,64,128]{3,2,1,0:T(8,128)} %get-tuple-element.35), channel_id=1, source_target_pairs={{0,2},{2,4},{4,6},{6,8},{8,10},{10,12},{12,14},{14,16},{16,18},{18... | collective-permute-start | bytes 589832 | tf_op jit(solution)/shard_map/ppermute | solution.py:22
  12.8 4.5 %collective-permute-start.5 = (f32[3,2,64,128]{3,2,1,0:T(8,128)S(1)}, f32[3,2,64,128]{3,2,1,0:T(8,128)}, u32[]{:S(2)}, u32[]{:S(2)}) collective-permute-start(f32[3,2,64,128]{3,2,1,0:T(8,128)S(1)} %get-tuple-element.34), channel_id=1, source_target_pairs={{2,0},{4,2},{6,4},{8,6},{10,8},{12,10},{14,12},{16,14},{18,16},{20... | collective-permute-start | bytes 589832 | tf_op jit(solution)/shard_map/ppermute | solution.py:23
  17.4 5.0 %sort.17 = (s32[1152]{0:T(1024)}, s32[1152]{0:T(1024)S(1)}) sort(s32[1152]{0:T(1024)S(1)} %get-tuple-element.63, s32[1152]{0:T(1024)S(1)} %iota.43), dimensions={0}, to_apply=%region_0.1 | sort | flops 12672 | bytes 18432 | tf_op jit(solution)/shard_map/jit(argsort)/sort | solution.py:152
  27.0 3.6 %convolution_bitcast_fusion = f32[3072,192]{0,1:T(8,128)} fusion(f32[3072,128]{1,0:T(8,128)S(1)} %bitcast.49, f32[192]{0:T(256)S(1)} %get-tuple-element.8, s32[192]{0:T(256)S(1)} %get-tuple-element.5), kind=kOutput, calls=%fused_computation.18 | convolution fusion | flops 906461184 | bytes 3933696 | tf_op jit(solution)/shard_map/dot_general | solution.py:165
  30.6 2.2 %copy.29 = f32[3072,192]{1,0:T(8,128)S(1)} copy(f32[3072,192]{0,1:T(8,128)} %convolution_bitcast_fusion) | data formatting | bytes 4718592
  37.2 40.4 %psum.7 = f32[3,1152]{1,0:T(4,128)S(1)} all-reduce(f32[3,1152]{1,0:T(4,128)S(1)} %fusion.77), channel_id=1, replica_groups=mesh['gy'=16,'gz'=2] {'gy','gz'}, use_global_device_ids=true, to_apply=%region_1.2 | all-reduce | flops 3456 | bytes 27648 | tf_op jit(solution)/shard_map/psum | solution.py:176
  83.4 1.7 %gather_fusion.4 = f32[192,3]{1,0:T(8,128)S(1)} fusion(f32[3,1152]{0,1:T(8,128)} %copy.17, s32[1024]{0:T(1024)S(1)} %pad_clamp_fusion), kind=kCustom, calls=%fused_computation.4 | custom fusion | bytes 5376 | tf_op jit(solution)/shard_map/gather | solution.py:178
  85.3 4.3 %fusion.93 = (f32[16,64,128]{2,1,0:T(8,128)}, f32[16,64,128]{2,1,0:T(8,128)}, f32[16,64,128]{2,1,0:T(8,128)}, f32[16,64,128]{2,1,0:T(8,128)}) fusion(f32[16,64,128]{2,1,0:T(8,128)} %get-tuple-element.22), kind=kLoop, calls=%fused_computation.199 | loop fusion | flops 9437184 | bytes 2621440 | tf_op jit(solution)/shard_map/jit(_where)/select_n | solution.py:32
  94.4 4.7 %collective-permute-start.3 = (f32[3,20,2,128]{3,2,1,0:T(2,128)S(1)}, f32[3,20,2,128]{3,2,1,0:T(2,128)S(1)}, u32[]{:S(2)}, u32[]{:S(2)}) collective-permute-start(f32[3,20,2,128]{3,2,1,0:T(2,128)S(1)} %get-tuple-element.14), channel_id=1, source_target_pairs={{1,0},{3,2},{5,4},{7,6},{9,8},{11,10},{13,12},{15,14},{17,16},{19,... | collective-permute-start | bytes 184328 | tf_op jit(solution)/shard_map/ppermute | solution.py:23
  103.3 4.5 %collective-permute-start.7 = (f32[3,20,2,128]{3,2,1,0:T(2,128)S(1)}, f32[3,20,2,128]{3,2,1,0:T(2,128)S(1)}, u32[]{:S(2)}, u32[]{:S(2)}) collective-permute-start(f32[3,20,2,128]{3,2,1,0:T(2,128)S(1)} %get-tuple-element.16), channel_id=1, source_target_pairs={{1,0},{3,2},{5,4},{7,6},{9,8},{11,10},{13,12},{15,14},{17,16},{19,... | collective-permute-start | bytes 184328 | tf_op jit(solution)/shard_map/ppermute | solution.py:23
  107.9 1.7 %pad_maximum_fusion = f32[3,20,68,128]{3,2,1,0:T(8,128)} fusion(f32[3,20,2,128]{3,2,1,0:T(2,128)S(1)} %collective-permute-done.3, f32[3,20,64,128]{3,2,1,0:T(8,128)S(1)} %get-tuple-element.53, f32[3,20,2,128]{3,2,1,0:T(2,128)S(1)} %collective-permute-done.2), kind=kLoop, calls=%fused_computation.23 | loop fusion | flops 1044480 | bytes 4177920 | tf_op jit(solution)/shard_map/concatenate | solution.py:24
  110.8 3.5 %select_maximum_fusion = f32[3,20,68,132]{3,2,1,0:T(8,128)} fusion(f32[3,20,2,128]{3,2,1,0:T(2,128)S(1)} %collective-permute-done.7, f32[3,20,64,128]{3,2,1,0:T(8,128)S(1)} %get-tuple-element.57, f32[3,20,2,128]{3,2,1,0:T(2,128)S(1)} %collective-permute-done.6), kind=kLoop, calls=%fused_computation.15 | loop fusion | flops 4308480 | bytes 4243200 | tf_op jit(solution)/shard_map/concatenate | solution.py:24
  114.4 20.4 %fusion.30 = f32[3,16,64,128]{3,2,1,0:T(8,128)} fusion(f32[3,16,64,128]{3,2,1,0:T(8,128)S(1)} %copy-done.2, f32[3,20,64,128]{3,2,1,0:T(8,128)} %copy-done.4, f32[3,20,2,128]{3,2,1,0:T(2,128)S(1)} %collective-permute-done.7, f32[3,20,2,128]{3,2,1,0:T(2,128)S(1)} %collective-permute-done.6, f32[3,20,64,128]{3,2,1,0:T(8,128)} %copy-done.3, ...), kind=kOutput, calls=%fused_computation.70 | convolution fusion | flops 929464320 | bytes 29947392 | tf_op jit(solution)/shard_map/dot_general | solution.py:180
  134.7 6.4 %fusion.48 = f32[3,16,64,128]{3,2,1,0:T(8,128)S(1)} fusion(f32[3,16,64,128]{3,2,1,0:T(8,128)} %fusion.30, f32[16,64,128]{2,1,0:T(8,128)} %get-tuple-element.49, f32[16,64,128]{2,1,0:T(8,128)} %get-tuple-element.48, f32[16,64,128]{2,1,0:T(8,128)S(1)} %copy-done.5, f32[16,64,128]{2,1,0:T(8,128)} %get-tuple-element.47, f32[16,64,128]{2,1,0:T(8,128)} %get-tuple-element.46), kind=kLoop, calls=%fused_computation.88 | loop fusion | flops 3538944 | bytes 5767168 | tf_op jit(solution)/shard_map/add | solution.py:73
  141.2 1.9 %collective-permute-start.8 = (f32[3,2,64,128]{3,2,1,0:T(8,128)S(1)}, f32[3,2,64,128]{3,2,1,0:T(8,128)S(1)}, u32[]{:S(2)}, u32[]{:S(2)}) collective-permute-start(f32[3,2,64,128]{3,2,1,0:T(8,128)S(1)} %get-tuple-element.19), channel_id=1, source_target_pairs={{2,0},{4,2},{6,4},{8,6},{10,8},{12,10},{14,12},{16,14},{18,16},{20... | collective-permute-start | bytes 589832 | tf_op jit(solution)/shard_map/ppermute | solution.py:23
  143.1 2.4 %collective-permute-start.9 = (f32[3,2,64,128]{3,2,1,0:T(8,128)S(1)}, f32[3,2,64,128]{3,2,1,0:T(8,128)S(1)}, u32[]{:S(2)}, u32[]{:S(2)}) collective-permute-start(f32[3,2,64,128]{3,2,1,0:T(8,128)S(1)} %get-tuple-element.20), channel_id=1, source_target_pairs={{0,2},{2,4},{4,6},{6,8},{8,10},{10,12},{12,14},{14,16},{16,18},{18... | collective-permute-start | bytes 589832 | tf_op jit(solution)/shard_map/ppermute | solution.py:22
  148.3 2.7 %collective-permute-done.9 = f32[3,2,64,128]{3,2,1,0:T(8,128)S(1)} collective-permute-done((f32[3,2,64,128]{3,2,1,0:T(8,128)S(1)}, f32[3,2,64,128]{3,2,1,0:T(8,128)S(1)}, u32[]{:S(2)}, u32[]{:S(2)}) %collective-permute-start.9) | collective-permute-done | bytes 196640 | tf_op jit(solution)/shard_map/ppermute | solution.py:22
  152.4 3.1 %collective-permute-start.10 = (f32[3,16,2,128]{3,2,1,0:T(2,128)S(1)}, f32[3,16,2,128]{3,2,1,0:T(2,128)S(1)}, u32[]{:S(2)}, u32[]{:S(2)}) collective-permute-start(f32[3,16,2,128]{3,2,1,0:T(2,128)S(1)} %get-tuple-element.17), channel_id=1, source_target_pairs={{1,0},{3,2},{5,4},{7,6},{9,8},{11,10},{13,12},{15,14},{17,16},{19,... | collective-permute-start | bytes 147464 | tf_op jit(solution)/shard_map/ppermute | solution.py:23
  158.5 3.0 %collective-permute-done.11 = f32[3,16,2,128]{3,2,1,0:T(2,128)S(1)} collective-permute-done((f32[3,16,2,128]{3,2,1,0:T(2,128)S(1)}, f32[3,16,2,128]{3,2,1,0:T(2,128)S(1)}, u32[]{:S(2)}, u32[]{:S(2)}) %collective-permute-start.11) | collective-permute-done | bytes 49184 | tf_op jit(solution)/shard_map/ppermute | solution.py:22
  161.5 2.1 %fusion.7 = f32[3,16,64,128]{3,2,1,0:T(8,128)} fusion(f32[3,16,2,128]{3,2,1,0:T(2,128)S(1)} %collective-permute-done.11, f32[3,16,64,128]{3,2,1,0:T(8,128)S(1)} %fusion.15, f32[3,16,2,128]{3,2,1,0:T(2,128)S(1)} %collective-permute-done.10, f32[16,64,128]{2,1,0:T(8,128)S(1)} %get-tuple-element.42, f32[16,64,128]{2,1,0:T(8,128)S(1)} %get-tuple-element.43, ...), kind=kLoop, calls=%fused_computation.47 | loop fusion | flops 5111808 | bytes 5865472 | tf_op jit(solution)/shard_map/add | solution.py:73
  (110 shorter events, 31.0 us)
Async XLA Ops:
  0.6 16.8 %copy-start.16 = (s32[1152]{0:T(1024)S(1)}, s32[1152]{0:T(1024)}, u32[]{:S(2)}) copy-start(s32[1152]{0:T(1024)} %param.10) | copy-start | bytes 13828
  0.6 23.3 %copy-start.12 = (s32[3,1152]{1,0:T(4,128)S(1)}, s32[3,1152]{1,0:T(4,128)}, u32[]{:S(2)}) copy-start(s32[3,1152]{1,0:T(4,128)} %param.11) | copy-start | bytes 41476
  2.5 22.8 %copy-start.13 = (f32[3,1152]{1,0:T(4,128)S(1)}, f32[3,1152]{1,0:T(4,128)}, u32[]{:S(2)}) copy-start(f32[3,1152]{1,0:T(4,128)} %param.12) | copy-start | bytes 41476
  2.5 87.8 %collective-permute-start = (f32[3,2,64,128]{3,2,1,0:T(8,128)}, f32[3,2,64,128]{3,2,1,0:T(8,128)}, u32[]{:S(2)}, u32[]{:S(2)}) collective-permute-start(f32[3,2,64,128]{3,2,1,0:T(8,128)} %get-tuple-element.33), channel_id=1, source_target_pairs={{0,2},{2,4},{4,6},{6,8},{8,10},{10,12},{12,14},{14,16},{16,18},{18... | collective-permute-start | bytes 589832 | tf_op jit(solution)/shard_map/ppermute | solution.py:22
  4.5 87.3 %collective-permute-start.1 = (f32[3,2,64,128]{3,2,1,0:T(8,128)}, f32[3,2,64,128]{3,2,1,0:T(8,128)}, u32[]{:S(2)}, u32[]{:S(2)}) collective-permute-start(f32[3,2,64,128]{3,2,1,0:T(8,128)} %get-tuple-element.32), channel_id=1, source_target_pairs={{2,0},{4,2},{6,4},{8,6},{10,8},{12,10},{14,12},{16,14},{18,16},{20... | collective-permute-start | bytes 589832 | tf_op jit(solution)/shard_map/ppermute | solution.py:23
  10.8 16.2 %copy-start = (f32[3,16,64,128]{3,2,1,0:T(8,128)S(1)}, f32[3,16,64,128]{3,2,1,0:T(8,128)}, u32[]{:S(2)}) copy-start(f32[3,16,64,128]{3,2,1,0:T(8,128)} %param.9) | copy-start | bytes 4718596
  10.8 88.3 %collective-permute-start.4 = (f32[3,2,64,128]{3,2,1,0:T(8,128)}, f32[3,2,64,128]{3,2,1,0:T(8,128)}, u32[]{:S(2)}, u32[]{:S(2)}) collective-permute-start(f32[3,2,64,128]{3,2,1,0:T(8,128)} %get-tuple-element.35), channel_id=1, source_target_pairs={{0,2},{2,4},{4,6},{6,8},{8,10},{10,12},{12,14},{14,16},{16,18},{18... | collective-permute-start | bytes 589832 | tf_op jit(solution)/shard_map/ppermute | solution.py:22
  12.8 87.8 %collective-permute-start.5 = (f32[3,2,64,128]{3,2,1,0:T(8,128)S(1)}, f32[3,2,64,128]{3,2,1,0:T(8,128)}, u32[]{:S(2)}, u32[]{:S(2)}) collective-permute-start(f32[3,2,64,128]{3,2,1,0:T(8,128)S(1)} %get-tuple-element.34), channel_id=1, source_target_pairs={{2,0},{4,2},{6,4},{8,6},{10,8},{12,10},{14,12},{16,14},{18,16},{20... | collective-permute-start | bytes 589832 | tf_op jit(solution)/shard_map/ppermute | solution.py:23
  33.4 44.9 %copy-start.14 = (f32[1152]{0:T(1024)S(1)}, f32[1152]{0:T(1024)}, u32[]{:S(2)}) copy-start(f32[1152]{0:T(1024)} %param.14) | copy-start | bytes 13828
  33.4 44.9 %copy-start.15 = (f32[1152]{0:T(1024)S(1)}, f32[1152]{0:T(1024)}, u32[]{:S(2)}) copy-start(f32[1152]{0:T(1024)} %param.13) | copy-start | bytes 13828
  33.4 45.3 %copy-start.2 = (f32[3,16,64,128]{3,2,1,0:T(8,128)S(1)}, f32[3,16,64,128]{3,2,1,0:T(8,128)}, u32[]{:S(2)}) copy-start(f32[3,16,64,128]{3,2,1,0:T(8,128)} %param.8) | copy-start | bytes 4718596
  93.0 16.6 %copy-start.3 = (f32[3,20,64,128]{3,2,1,0:T(8,128)}, f32[3,20,64,128]{3,2,1,0:T(8,128)S(1)}, u32[]{:S(2)}) copy-start(f32[3,20,64,128]{3,2,1,0:T(8,128)S(1)} %get-tuple-element.53) | copy-start | bytes 5898244
  93.1 14.8 %collective-permute-start.2 = (f32[3,20,2,128]{3,2,1,0:T(2,128)S(1)}, f32[3,20,2,128]{3,2,1,0:T(2,128)S(1)}, u32[]{:S(2)}, u32[]{:S(2)}) collective-permute-start(f32[3,20,2,128]{3,2,1,0:T(2,128)S(1)} %get-tuple-element.13), channel_id=1, source_target_pairs={{0,1},{2,3},{4,5},{6,7},{8,9},{10,11},{12,13},{14,15},{16,17},{18,... | collective-permute-start | bytes 184328 | tf_op jit(solution)/shard_map/ppermute | solution.py:22
  94.4 13.5 %collective-permute-start.3 = (f32[3,20,2,128]{3,2,1,0:T(2,128)S(1)}, f32[3,20,2,128]{3,2,1,0:T(2,128)S(1)}, u32[]{:S(2)}, u32[]{:S(2)}) collective-permute-start(f32[3,20,2,128]{3,2,1,0:T(2,128)S(1)} %get-tuple-element.14), channel_id=1, source_target_pairs={{1,0},{3,2},{5,4},{7,6},{9,8},{11,10},{13,12},{15,14},{17,16},{19,... | collective-permute-start | bytes 184328 | tf_op jit(solution)/shard_map/ppermute | solution.py:23
  100.7 13.7 %copy-start.11 = (f32[3,18,64,128]{3,2,1,0:T(8,128)}, f32[3,18,64,128]{3,2,1,0:T(8,128)S(1)}, u32[]{:S(2)}) copy-start(f32[3,18,64,128]{3,2,1,0:T(8,128)S(1)} %get-tuple-element.29) | copy-start | bytes 5308420
  101.9 7.7 %copy-start.7 = (f32[3,18,64,128]{3,2,1,0:T(8,128)}, f32[3,18,64,128]{3,2,1,0:T(8,128)S(1)}, u32[]{:S(2)}) copy-start(f32[3,18,64,128]{3,2,1,0:T(8,128)S(1)} %get-tuple-element.56) | copy-start | bytes 5308420
  101.9 8.9 %copy-start.4 = (f32[3,20,64,128]{3,2,1,0:T(8,128)}, f32[3,20,64,128]{3,2,1,0:T(8,128)S(1)}, u32[]{:S(2)}) copy-start(f32[3,20,64,128]{3,2,1,0:T(8,128)S(1)} %get-tuple-element.57) | copy-start | bytes 5898244
  102.0 8.8 %collective-permute-start.6 = (f32[3,20,2,128]{3,2,1,0:T(2,128)S(1)}, f32[3,20,2,128]{3,2,1,0:T(2,128)S(1)}, u32[]{:S(2)}, u32[]{:S(2)}) collective-permute-start(f32[3,20,2,128]{3,2,1,0:T(2,128)S(1)} %get-tuple-element.15), channel_id=1, source_target_pairs={{0,1},{2,3},{4,5},{6,7},{8,9},{10,11},{12,13},{14,15},{16,17},{18,... | collective-permute-start | bytes 184328 | tf_op jit(solution)/shard_map/ppermute | solution.py:22
  103.3 7.5 %collective-permute-start.7 = (f32[3,20,2,128]{3,2,1,0:T(2,128)S(1)}, f32[3,20,2,128]{3,2,1,0:T(2,128)S(1)}, u32[]{:S(2)}, u32[]{:S(2)}) collective-permute-start(f32[3,20,2,128]{3,2,1,0:T(2,128)S(1)} %get-tuple-element.16), channel_id=1, source_target_pairs={{1,0},{3,2},{5,4},{7,6},{9,8},{11,10},{13,12},{15,14},{17,16},{19,... | collective-permute-start | bytes 184328 | tf_op jit(solution)/shard_map/ppermute | solution.py:23
  114.4 20.4 %copy-start.5 = (f32[16,64,128]{2,1,0:T(8,128)S(1)}, f32[16,64,128]{2,1,0:T(8,128)}, u32[]{:S(2)}) copy-start(f32[16,64,128]{2,1,0:T(8,128)} %get-tuple-element.21) | copy-start | bytes 1572868
  141.2 7.1 %collective-permute-start.8 = (f32[3,2,64,128]{3,2,1,0:T(8,128)S(1)}, f32[3,2,64,128]{3,2,1,0:T(8,128)S(1)}, u32[]{:S(2)}, u32[]{:S(2)}) collective-permute-start(f32[3,2,64,128]{3,2,1,0:T(8,128)S(1)} %get-tuple-element.19), channel_id=1, source_target_pairs={{2,0},{4,2},{6,4},{8,6},{10,8},{12,10},{14,12},{16,14},{18,16},{20... | collective-permute-start | bytes 589832 | tf_op jit(solution)/shard_map/ppermute | solution.py:23
  143.1 7.9 %collective-permute-start.9 = (f32[3,2,64,128]{3,2,1,0:T(8,128)S(1)}, f32[3,2,64,128]{3,2,1,0:T(8,128)S(1)}, u32[]{:S(2)}, u32[]{:S(2)}) collective-permute-start(f32[3,2,64,128]{3,2,1,0:T(8,128)S(1)} %get-tuple-element.20), channel_id=1, source_target_pairs={{0,2},{2,4},{4,6},{6,8},{8,10},{10,12},{12,14},{14,16},{16,18},{18... | collective-permute-start | bytes 589832 | tf_op jit(solution)/shard_map/ppermute | solution.py:22
  152.4 6.1 %collective-permute-start.10 = (f32[3,16,2,128]{3,2,1,0:T(2,128)S(1)}, f32[3,16,2,128]{3,2,1,0:T(2,128)S(1)}, u32[]{:S(2)}, u32[]{:S(2)}) collective-permute-start(f32[3,16,2,128]{3,2,1,0:T(2,128)S(1)} %get-tuple-element.17), channel_id=1, source_target_pairs={{1,0},{3,2},{5,4},{7,6},{9,8},{11,10},{13,12},{15,14},{17,16},{19,... | collective-permute-start | bytes 147464 | tf_op jit(solution)/shard_map/ppermute | solution.py:23
  155.5 6.0 %collective-permute-start.11 = (f32[3,16,2,128]{3,2,1,0:T(2,128)S(1)}, f32[3,16,2,128]{3,2,1,0:T(2,128)S(1)}, u32[]{:S(2)}, u32[]{:S(2)}) collective-permute-start(f32[3,16,2,128]{3,2,1,0:T(2,128)S(1)} %get-tuple-element.18), channel_id=1, source_target_pairs={{0,1},{2,3},{4,5},{6,7},{8,9},{10,11},{12,13},{14,15},{16,17},{18,... | collective-permute-start | bytes 147464 | tf_op jit(solution)/shard_map/ppermute | solution.py:22
  (9 other events, 35.2 us)
where the time goes:
time: 164 us
  blocking collectives  40.4 us (25%)
  starting transfers between devices  33.8 us (21%)
  other arithmetic  33.1 us (20%)
  matrix products  25.8 us (16%)
  local copies, waits for them, and re-layouts  22.7 us (14%)
  waiting for transfers between devices  5.74 us (4%)
  between operations  1.99 us (1%)
    psum x1, blocking collectives, on_device(): point_velocity = lax.psum(partial_velocity, ('gy', 'gz'))  40.4 us
    ppermute x6, starting transfers between devices, with_halo(): after = lax.ppermute(initial, axis, down)  23.4 us
    dot_general x1, matrix products, on_device(): jnp.dot(spread.reshape(-1, spread.shape[3]), table_x.T, precision=highest...  20.4 us
    ppermute x6, starting transfers between devices, with_halo(): before = lax.ppermute(last, axis, up)  10.4 us
    add x3, other arithmetic, remesh_padded(): total = total + remesh_kernel(offset - moved)[None] * part  9.8 us
    select_n x4, other arithmetic, remesh_kernel(): return jnp.where(mag < 1.0, inner, jnp.where(mag < 2.0, outer, 0.0))  7.58 us
    unnamed x47, local copies, waits for them, and re-layouts  6.02 us
    ppermute x6, waiting for transfers between devices, with_halo(): before = lax.ppermute(last, axis, up)  5.72 us
  transfers between devices with their start and end apart: 12, of which 2 were waited for; matrix products, arithmetic and copies ran while one was open for 27% of the time, Pallas kernels for 0%

commit v1 on v0

--- a/solution.py
+++ b/solution.py
@@ -173,7 +173,8 @@
     partial_velocity = jnp.dot(
         compact, selector, precision=highest, preferred_element_type=jnp.float32
     )
-    point_velocity = lax.psum(partial_velocity, ("gy", "gz"))
+    partial = lax.psum(partial_velocity, "gz")
+    point_velocity = lax.psum(partial, "gy")
     sources = blade_forces(point_velocity, chord, twist, angle_step)
     local_sources = sources[:, picked]
     spread = jnp.einsum("cq,yq,zq->cyzq", local_sources, table_y, table_z, precision=highest)

time: 164 us -> 187 us (1.14)
  the two profiles are of different devices: /device:TPU:10 before, /device:TPU:6 now
where the time goes in v1:
time: 187 us; the launch traced here: 186 us
  blocking collectives  61.9 us (33%)
  other arithmetic  33.2 us (18%)
  starting transfers between devices  32 us (17%)
  matrix products  26 us (14%)
  local copies, waits for them, and re-layouts  22.8 us (12%)
  waiting for transfers between devices  8.16 us (4%)
  between operations  1.99 us (1%)
    psum x1, blocking collectives, on_device(): point_velocity = lax.psum(partial, 'gy')  54.6 us
    ppermute x6, starting transfers between devices, with_halo(): after = lax.ppermute(initial, axis, down)  21.6 us
    dot_general x1, matrix products, on_device(): jnp.dot(spread.reshape(-1, spread.shape[3]), table_x.T, precision=highest...  20.6 us
    ppermute x6, starting transfers between devices, with_halo(): before = lax.ppermute(last, axis, up)  10.4 us
    add x3, other arithmetic, remesh_padded(): total = total + remesh_kernel(offset - moved)[None] * part  9.82 us
    ppermute x6, waiting for transfers between devices, with_halo(): before = lax.ppermute(last, axis, up)  8.15 us
    select_n x4, other arithmetic, remesh_kernel(): return jnp.where(mag < 1.0, inner, jnp.where(mag < 2.0, outer, 0.0))  7.59 us
    psum x1, blocking collectives, on_device(): partial = lax.psum(partial_velocity, 'gz')  7.32 us
  transfers between devices with their start and end apart: 12, of which 2 were waited for; matrix products, arithmetic and copies ran while one was open for 24% of the time, Pallas kernels for 0%

profile of v1, /device:TPU:6, one launch (start us, length us, event | category | flops | bytes accessed | tf_op | source)
XLA Modules:
  0.0 185.9 jit_solution(11465948127642026870)
XLA Ops:
  0.6 1.8 fusion.252
  2.5 2.0 %collective-permute-start = (f32[3,2,64,128]{3,2,1,0:T(8,128)}, f32[3,2,64,128]{3,2,1,0:T(8,128)}, u32[]{:S(2)}, u32[]{:S(2)}) collective-permute-start(f32[3,2,64,128]{3,2,1,0:T(8,128)} %get-tuple-element.33), channel_id=1, source_target_pairs={{0,2},{2,4},{4,6},{6,8},{8,10},{10,12},{12,14},{14,16},{16,18},{18... | collective-permute-start | bytes 589832 | tf_op jit(solution)/shard_map/ppermute | solution.py:22
  4.5 3.6 %collective-permute-start.1 = (f32[3,2,64,128]{3,2,1,0:T(8,128)}, f32[3,2,64,128]{3,2,1,0:T(8,128)}, u32[]{:S(2)}, u32[]{:S(2)}) collective-permute-start(f32[3,2,64,128]{3,2,1,0:T(8,128)} %get-tuple-element.32), channel_id=1, source_target_pairs={{2,0},{4,2},{6,4},{8,6},{10,8},{12,10},{14,12},{16,14},{18,16},{20... | collective-permute-start | bytes 589832 | tf_op jit(solution)/shard_map/ppermute | solution.py:23
  9.9 2.0 %collective-permute-start.4 = (f32[3,2,64,128]{3,2,1,0:T(8,128)}, f32[3,2,64,128]{3,2,1,0:T(8,128)}, u32[]{:S(2)}, u32[]{:S(2)}) collective-permute-start(f32[3,2,64,128]{3,2,1,0:T(8,128)} %get-tuple-element.35), channel_id=1, source_target_pairs={{0,2},{2,4},{4,6},{6,8},{8,10},{10,12},{12,14},{14,16},{16,18},{18... | collective-permute-start | bytes 589832 | tf_op jit(solution)/shard_map/ppermute | solution.py:22
  11.9 3.6 %collective-permute-start.5 = (f32[3,2,64,128]{3,2,1,0:T(8,128)S(1)}, f32[3,2,64,128]{3,2,1,0:T(8,128)}, u32[]{:S(2)}, u32[]{:S(2)}) collective-permute-start(f32[3,2,64,128]{3,2,1,0:T(8,128)S(1)} %get-tuple-element.34), channel_id=1, source_target_pairs={{2,0},{4,2},{6,4},{8,6},{10,8},{12,10},{14,12},{16,14},{18,16},{20... | collective-permute-start | bytes 589832 | tf_op jit(solution)/shard_map/ppermute | solution.py:23
  15.7 5.0 %sort.17 = (s32[1152]{0:T(1024)}, s32[1152]{0:T(1024)S(1)}) sort(s32[1152]{0:T(1024)S(1)} %get-tuple-element.63, s32[1152]{0:T(1024)S(1)} %iota.43), dimensions={0}, to_apply=%region_0.1 | sort | flops 12672 | bytes 18432 | tf_op jit(solution)/shard_map/jit(argsort)/sort | solution.py:152
  25.3 3.5 %convolution_bitcast_fusion = f32[3072,192]{0,1:T(8,128)} fusion(f32[3072,128]{1,0:T(8,128)S(1)} %bitcast.49, f32[192]{0:T(256)S(1)} %get-tuple-element.8, s32[192]{0:T(256)S(1)} %get-tuple-element.5), kind=kOutput, calls=%fused_computation.18 | convolution fusion | flops 906461184 | bytes 3933696 | tf_op jit(solution)/shard_map/dot_general | solution.py:165
  28.8 2.2 %copy.29 = f32[3072,192]{1,0:T(8,128)S(1)} copy(f32[3072,192]{0,1:T(8,128)} %convolution_bitcast_fusion) | data formatting | bytes 4718592
  35.4 7.3 %psum.14 = f32[3,1152]{1,0:T(4,128)S(1)} all-reduce(f32[3,1152]{1,0:T(4,128)S(1)} %fusion.77), channel_id=1, replica_groups=mesh['gy'=16,'gz'=2] {'gz'}, use_global_device_ids=true, to_apply=%region_1.2 | all-reduce | flops 3456 | bytes 27648 | tf_op jit(solution)/shard_map/psum | solution.py:176
  42.7 54.6 %psum.15 = f32[3,1152]{1,0:T(4,128)S(1)} all-reduce(f32[3,1152]{1,0:T(4,128)S(1)} %psum.14), channel_id=1, replica_groups=mesh['gy'=16,'gz'=2] {'gy'}, use_global_device_ids=true, to_apply=%region_2.3 | all-reduce | flops 3456 | bytes 27648 | tf_op jit(solution)/shard_map/psum | solution.py:177
  103.2 1.7 gather_fusion.4
  105.0 4.3 %fusion.93 = (f32[16,64,128]{2,1,0:T(8,128)}, f32[16,64,128]{2,1,0:T(8,128)}, f32[16,64,128]{2,1,0:T(8,128)}, f32[16,64,128]{2,1,0:T(8,128)}) fusion(f32[16,64,128]{2,1,0:T(8,128)} %get-tuple-element.22), kind=kLoop, calls=%fused_computation.199 | loop fusion | flops 9437184 | bytes 2621440 | tf_op jit(solution)/shard_map/jit(_where)/select_n | solution.py:32
  114.1 4.7 %collective-permute-start.3 = (f32[3,20,2,128]{3,2,1,0:T(2,128)S(1)}, f32[3,20,2,128]{3,2,1,0:T(2,128)S(1)}, u32[]{:S(2)}, u32[]{:S(2)}) collective-permute-start(f32[3,20,2,128]{3,2,1,0:T(2,128)S(1)} %get-tuple-element.14), channel_id=1, source_target_pairs={{1,0},{3,2},{5,4},{7,6},{9,8},{11,10},{13,12},{15,14},{17,16},{19,... | collective-permute-start | bytes 184328 | tf_op jit(solution)/shard_map/ppermute | solution.py:23
  123.0 4.5 %collective-permute-start.7 = (f32[3,20,2,128]{3,2,1,0:T(2,128)S(1)}, f32[3,20,2,128]{3,2,1,0:T(2,128)S(1)}, u32[]{:S(2)}, u32[]{:S(2)}) collective-permute-start(f32[3,20,2,128]{3,2,1,0:T(2,128)S(1)} %get-tuple-element.16), channel_id=1, source_target_pairs={{1,0},{3,2},{5,4},{7,6},{9,8},{11,10},{13,12},{15,14},{17,16},{19,... | collective-permute-start | bytes 184328 | tf_op jit(solution)/shard_map/ppermute | solution.py:23
  127.6 1.7 pad_maximum_fusion
  130.6 3.5 %select_maximum_fusion = f32[3,20,68,132]{3,2,1,0:T(8,128)} fusion(f32[3,20,2,128]{3,2,1,0:T(2,128)S(1)} %collective-permute-done.7, f32[3,20,64,128]{3,2,1,0:T(8,128)S(1)} %get-tuple-element.57, f32[3,20,2,128]{3,2,1,0:T(2,128)S(1)} %collective-permute-done.6), kind=kLoop, calls=%fused_computation.15 | loop fusion | flops 4308480 | bytes 4243200 | tf_op jit(solution)/shard_map/concatenate | solution.py:24
  134.1 20.6 %fusion.30 = f32[3,16,64,128]{3,2,1,0:T(8,128)} fusion(f32[3,16,64,128]{3,2,1,0:T(8,128)S(1)} %copy-done.2, f32[3,20,64,128]{3,2,1,0:T(8,128)} %copy-done.4, f32[3,20,2,128]{3,2,1,0:T(2,128)S(1)} %collective-permute-done.7, f32[3,20,2,128]{3,2,1,0:T(2,128)S(1)} %collective-permute-done.6, f32[3,20,64,128]{3,2,1,0:T(8,128)} %copy-done.3, ...), kind=kOutput, calls=%fused_computation.70 | convolution fusion | flops 929464320 | bytes 29947392 | tf_op jit(solution)/shard_map/dot_general | solution.py:181
  154.7 6.4 %fusion.48 = f32[3,16,64,128]{3,2,1,0:T(8,128)S(1)} fusion(f32[3,16,64,128]{3,2,1,0:T(8,128)} %fusion.30, f32[16,64,128]{2,1,0:T(8,128)} %get-tuple-element.49, f32[16,64,128]{2,1,0:T(8,128)} %get-tuple-element.48, f32[16,64,128]{2,1,0:T(8,128)S(1)} %copy-done.5, f32[16,64,128]{2,1,0:T(8,128)} %get-tuple-element.47, f32[16,64,128]{2,1,0:T(8,128)} %get-tuple-element.46), kind=kLoop, calls=%fused_computation.88 | loop fusion | flops 3538944 | bytes 5767168 | tf_op jit(solution)/shard_map/add | solution.py:73
  161.1 1.9 %collective-permute-start.8 = (f32[3,2,64,128]{3,2,1,0:T(8,128)S(1)}, f32[3,2,64,128]{3,2,1,0:T(8,128)S(1)}, u32[]{:S(2)}, u32[]{:S(2)}) collective-permute-start(f32[3,2,64,128]{3,2,1,0:T(8,128)S(1)} %get-tuple-element.19), channel_id=1, source_target_pairs={{2,0},{4,2},{6,4},{8,6},{10,8},{12,10},{14,12},{16,14},{18,16},{20... | collective-permute-start | bytes 589832 | tf_op jit(solution)/shard_map/ppermute | solution.py:23
  163.1 2.4 %collective-permute-start.9 = (f32[3,2,64,128]{3,2,1,0:T(8,128)S(1)}, f32[3,2,64,128]{3,2,1,0:T(8,128)S(1)}, u32[]{:S(2)}, u32[]{:S(2)}) collective-permute-start(f32[3,2,64,128]{3,2,1,0:T(8,128)S(1)} %get-tuple-element.20), channel_id=1, source_target_pairs={{0,2},{2,4},{4,6},{6,8},{8,10},{10,12},{12,14},{14,16},{16,18},{18... | collective-permute-start | bytes 589832 | tf_op jit(solution)/shard_map/ppermute | solution.py:22
  168.3 5.1 %collective-permute-done.9 = f32[3,2,64,128]{3,2,1,0:T(8,128)S(1)} collective-permute-done((f32[3,2,64,128]{3,2,1,0:T(8,128)S(1)}, f32[3,2,64,128]{3,2,1,0:T(8,128)S(1)}, u32[]{:S(2)}, u32[]{:S(2)}) %collective-permute-start.9) | collective-permute-done | bytes 196640 | tf_op jit(solution)/shard_map/ppermute | solution.py:22
  174.8 3.1 %collective-permute-start.10 = (f32[3,16,2,128]{3,2,1,0:T(2,128)S(1)}, f32[3,16,2,128]{3,2,1,0:T(2,128)S(1)}, u32[]{:S(2)}, u32[]{:S(2)}) collective-permute-start(f32[3,16,2,128]{3,2,1,0:T(2,128)S(1)} %get-tuple-element.17), channel_id=1, source_target_pairs={{1,0},{3,2},{5,4},{7,6},{9,8},{11,10},{13,12},{15,14},{17,16},{19,... | collective-permute-start | bytes 147464 | tf_op jit(solution)/shard_map/ppermute | solution.py:23
  180.8 3.0 %collective-permute-done.11 = f32[3,16,2,128]{3,2,1,0:T(2,128)S(1)} collective-permute-done((f32[3,16,2,128]{3,2,1,0:T(2,128)S(1)}, f32[3,16,2,128]{3,2,1,0:T(2,128)S(1)}, u32[]{:S(2)}, u32[]{:S(2)}) %collective-permute-start.11) | collective-permute-done | bytes 49184 | tf_op jit(solution)/shard_map/ppermute | solution.py:22
  183.9 2.1 %fusion.7 = f32[3,16,64,128]{3,2,1,0:T(8,128)} fusion(f32[3,16,2,128]{3,2,1,0:T(2,128)S(1)} %collective-permute-done.11, f32[3,16,64,128]{3,2,1,0:T(8,128)S(1)} %fusion.15, f32[3,16,2,128]{3,2,1,0:T(2,128)S(1)} %collective-permute-done.10, f32[16,64,128]{2,1,0:T(8,128)S(1)} %get-tuple-element.42, f32[16,64,128]{2,1,0:T(8,128)S(1)} %get-tuple-element.43, ...), kind=kLoop, calls=%fused_computation.47 | loop fusion | flops 5111808 | bytes 5865472 | tf_op jit(solution)/shard_map/add | solution.py:73
  (111 shorter events, 32.8 us)
Async XLA Ops:
  0.6 15.0 %copy-start.16 = (s32[1152]{0:T(1024)S(1)}, s32[1152]{0:T(1024)}, u32[]{:S(2)}) copy-start(s32[1152]{0:T(1024)} %param.10) | copy-start | bytes 13828
  0.6 21.5 %copy-start.12 = (s32[3,1152]{1,0:T(4,128)S(1)}, s32[3,1152]{1,0:T(4,128)}, u32[]{:S(2)}) copy-start(s32[3,1152]{1,0:T(4,128)} %param.11) | copy-start | bytes 41476
  2.5 21.0 %copy-start.13 = (f32[3,1152]{1,0:T(4,128)S(1)}, f32[3,1152]{1,0:T(4,128)}, u32[]{:S(2)}) copy-start(f32[3,1152]{1,0:T(4,128)} %param.12) | copy-start | bytes 41476
  2.5 107.5 %collective-permute-start = (f32[3,2,64,128]{3,2,1,0:T(8,128)}, f32[3,2,64,128]{3,2,1,0:T(8,128)}, u32[]{:S(2)}, u32[]{:S(2)}) collective-permute-start(f32[3,2,64,128]{3,2,1,0:T(8,128)} %get-tuple-element.33), channel_id=1, source_target_pairs={{0,2},{2,4},{4,6},{6,8},{8,10},{10,12},{12,14},{14,16},{16,18},{18... | collective-permute-start | bytes 589832 | tf_op jit(solution)/shard_map/ppermute | solution.py:22
  4.5 107.0 %collective-permute-start.1 = (f32[3,2,64,128]{3,2,1,0:T(8,128)}, f32[3,2,64,128]{3,2,1,0:T(8,128)}, u32[]{:S(2)}, u32[]{:S(2)}) collective-permute-start(f32[3,2,64,128]{3,2,1,0:T(8,128)} %get-tuple-element.32), channel_id=1, source_target_pairs={{2,0},{4,2},{6,4},{8,6},{10,8},{12,10},{14,12},{16,14},{18,16},{20... | collective-permute-start | bytes 589832 | tf_op jit(solution)/shard_map/ppermute | solution.py:23
  9.9 15.4 %copy-start = (f32[3,16,64,128]{3,2,1,0:T(8,128)S(1)}, f32[3,16,64,128]{3,2,1,0:T(8,128)}, u32[]{:S(2)}) copy-start(f32[3,16,64,128]{3,2,1,0:T(8,128)} %param.9) | copy-start | bytes 4718596
  9.9 108.9 %collective-permute-start.4 = (f32[3,2,64,128]{3,2,1,0:T(8,128)}, f32[3,2,64,128]{3,2,1,0:T(8,128)}, u32[]{:S(2)}, u32[]{:S(2)}) collective-permute-start(f32[3,2,64,128]{3,2,1,0:T(8,128)} %get-tuple-element.35), channel_id=1, source_target_pairs={{0,2},{2,4},{4,6},{6,8},{8,10},{10,12},{12,14},{14,16},{16,18},{18... | collective-permute-start | bytes 589832 | tf_op jit(solution)/shard_map/ppermute | solution.py:22
  11.9 108.5 %collective-permute-start.5 = (f32[3,2,64,128]{3,2,1,0:T(8,128)S(1)}, f32[3,2,64,128]{3,2,1,0:T(8,128)}, u32[]{:S(2)}, u32[]{:S(2)}) collective-permute-start(f32[3,2,64,128]{3,2,1,0:T(8,128)S(1)} %get-tuple-element.34), channel_id=1, source_target_pairs={{2,0},{4,2},{6,4},{8,6},{10,8},{12,10},{14,12},{16,14},{18,16},{20... | collective-permute-start | bytes 589832 | tf_op jit(solution)/shard_map/ppermute | solution.py:23
  31.6 66.4 %copy-start.14 = (f32[1152]{0:T(1024)S(1)}, f32[1152]{0:T(1024)}, u32[]{:S(2)}) copy-start(f32[1152]{0:T(1024)} %param.14) | copy-start | bytes 13828
  31.6 66.4 %copy-start.15 = (f32[1152]{0:T(1024)S(1)}, f32[1152]{0:T(1024)}, u32[]{:S(2)}) copy-start(f32[1152]{0:T(1024)} %param.13) | copy-start | bytes 13828
  31.6 66.8 %copy-start.2 = (f32[3,16,64,128]{3,2,1,0:T(8,128)S(1)}, f32[3,16,64,128]{3,2,1,0:T(8,128)}, u32[]{:S(2)}) copy-start(f32[3,16,64,128]{3,2,1,0:T(8,128)} %param.8) | copy-start | bytes 4718596
  112.7 16.6 %copy-start.3 = (f32[3,20,64,128]{3,2,1,0:T(8,128)}, f32[3,20,64,128]{3,2,1,0:T(8,128)S(1)}, u32[]{:S(2)}) copy-start(f32[3,20,64,128]{3,2,1,0:T(8,128)S(1)} %get-tuple-element.53) | copy-start | bytes 5898244
  112.8 14.8 %collective-permute-start.2 = (f32[3,20,2,128]{3,2,1,0:T(2,128)S(1)}, f32[3,20,2,128]{3,2,1,0:T(2,128)S(1)}, u32[]{:S(2)}, u32[]{:S(2)}) collective-permute-start(f32[3,20,2,128]{3,2,1,0:T(2,128)S(1)} %get-tuple-element.13), channel_id=1, source_target_pairs={{0,1},{2,3},{4,5},{6,7},{8,9},{10,11},{12,13},{14,15},{16,17},{18,... | collective-permute-start | bytes 184328 | tf_op jit(solution)/shard_map/ppermute | solution.py:22
  114.1 13.5 %collective-permute-start.3 = (f32[3,20,2,128]{3,2,1,0:T(2,128)S(1)}, f32[3,20,2,128]{3,2,1,0:T(2,128)S(1)}, u32[]{:S(2)}, u32[]{:S(2)}) collective-permute-start(f32[3,20,2,128]{3,2,1,0:T(2,128)S(1)} %get-tuple-element.14), channel_id=1, source_target_pairs={{1,0},{3,2},{5,4},{7,6},{9,8},{11,10},{13,12},{15,14},{17,16},{19,... | collective-permute-start | bytes 184328 | tf_op jit(solution)/shard_map/ppermute | solution.py:23
  120.4 13.7 %copy-start.11 = (f32[3,18,64,128]{3,2,1,0:T(8,128)}, f32[3,18,64,128]{3,2,1,0:T(8,128)S(1)}, u32[]{:S(2)}) copy-start(f32[3,18,64,128]{3,2,1,0:T(8,128)S(1)} %get-tuple-element.29) | copy-start | bytes 5308420
  121.6 7.7 %copy-start.7 = (f32[3,18,64,128]{3,2,1,0:T(8,128)}, f32[3,18,64,128]{3,2,1,0:T(8,128)S(1)}, u32[]{:S(2)}) copy-start(f32[3,18,64,128]{3,2,1,0:T(8,128)S(1)} %get-tuple-element.56) | copy-start | bytes 5308420
  121.6 8.9 %copy-start.4 = (f32[3,20,64,128]{3,2,1,0:T(8,128)}, f32[3,20,64,128]{3,2,1,0:T(8,128)S(1)}, u32[]{:S(2)}) copy-start(f32[3,20,64,128]{3,2,1,0:T(8,128)S(1)} %get-tuple-element.57) | copy-start | bytes 5898244
  121.7 8.8 %collective-permute-start.6 = (f32[3,20,2,128]{3,2,1,0:T(2,128)S(1)}, f32[3,20,2,128]{3,2,1,0:T(2,128)S(1)}, u32[]{:S(2)}, u32[]{:S(2)}) collective-permute-start(f32[3,20,2,128]{3,2,1,0:T(2,128)S(1)} %get-tuple-element.15), channel_id=1, source_target_pairs={{0,1},{2,3},{4,5},{6,7},{8,9},{10,11},{12,13},{14,15},{16,17},{18,... | collective-permute-start | bytes 184328 | tf_op jit(solution)/shard_map/ppermute | solution.py:22
  123.0 7.5 %collective-permute-start.7 = (f32[3,20,2,128]{3,2,1,0:T(2,128)S(1)}, f32[3,20,2,128]{3,2,1,0:T(2,128)S(1)}, u32[]{:S(2)}, u32[]{:S(2)}) collective-permute-start(f32[3,20,2,128]{3,2,1,0:T(2,128)S(1)} %get-tuple-element.16), channel_id=1, source_target_pairs={{1,0},{3,2},{5,4},{7,6},{9,8},{11,10},{13,12},{15,14},{17,16},{19,... | collective-permute-start | bytes 184328 | tf_op jit(solution)/shard_map/ppermute | solution.py:23
  134.1 20.6 %copy-start.5 = (f32[16,64,128]{2,1,0:T(8,128)S(1)}, f32[16,64,128]{2,1,0:T(8,128)}, u32[]{:S(2)}) copy-start(f32[16,64,128]{2,1,0:T(8,128)} %get-tuple-element.21) | copy-start | bytes 1572868
  161.1 7.1 %collective-permute-start.8 = (f32[3,2,64,128]{3,2,1,0:T(8,128)S(1)}, f32[3,2,64,128]{3,2,1,0:T(8,128)S(1)}, u32[]{:S(2)}, u32[]{:S(2)}) collective-permute-start(f32[3,2,64,128]{3,2,1,0:T(8,128)S(1)} %get-tuple-element.19), channel_id=1, source_target_pairs={{2,0},{4,2},{6,4},{8,6},{10,8},{12,10},{14,12},{16,14},{18,16},{20... | collective-permute-start | bytes 589832 | tf_op jit(solution)/shard_map/ppermute | solution.py:23
  163.1 10.3 %collective-permute-start.9 = (f32[3,2,64,128]{3,2,1,0:T(8,128)S(1)}, f32[3,2,64,128]{3,2,1,0:T(8,128)S(1)}, u32[]{:S(2)}, u32[]{:S(2)}) collective-permute-start(f32[3,2,64,128]{3,2,1,0:T(8,128)S(1)} %get-tuple-element.20), channel_id=1, source_target_pairs={{0,2},{2,4},{4,6},{6,8},{8,10},{10,12},{12,14},{14,16},{16,18},{18... | collective-permute-start | bytes 589832 | tf_op jit(solution)/shard_map/ppermute | solution.py:22
  174.8 6.1 %collective-permute-start.10 = (f32[3,16,2,128]{3,2,1,0:T(2,128)S(1)}, f32[3,16,2,128]{3,2,1,0:T(2,128)S(1)}, u32[]{:S(2)}, u32[]{:S(2)}) collective-permute-start(f32[3,16,2,128]{3,2,1,0:T(2,128)S(1)} %get-tuple-element.17), channel_id=1, source_target_pairs={{1,0},{3,2},{5,4},{7,6},{9,8},{11,10},{13,12},{15,14},{17,16},{19,... | collective-permute-start | bytes 147464 | tf_op jit(solution)/shard_map/ppermute | solution.py:23
  177.9 6.0 %collective-permute-start.11 = (f32[3,16,2,128]{3,2,1,0:T(2,128)S(1)}, f32[3,16,2,128]{3,2,1,0:T(2,128)S(1)}, u32[]{:S(2)}, u32[]{:S(2)}) collective-permute-start(f32[3,16,2,128]{3,2,1,0:T(2,128)S(1)} %get-tuple-element.18), channel_id=1, source_target_pairs={{0,1},{2,3},{4,5},{6,7},{8,9},{10,11},{12,13},{14,15},{16,17},{18,... | collective-permute-start | bytes 147464 | tf_op jit(solution)/shard_map/ppermute | solution.py:22
  (9 other events, 35.2 us)
